TPU v7x, 32 devices: a whole 2x2x4 slice. The times are simulated.
32 devices in a mesh: gx: 4 (over y, x), gy: 2 (over core), gz: 4 (over z).
Axes of the slice: x: 2, y: 2, z: 4, core: 2. Of those that a mesh axis runs over, the one named last changes fastest.
Arguments:
- labels: int32 [128, 128, 512], P('gx', 'gy', 'gz'), may hold values from 0 to 7
- conductivity: float32 [7, 8], replicated, may hold values from -0.08 to 2, as said below
- right_side: float32 [128, 128, 512], P('gx', 'gy', 'gz'), may hold values from -18 to 18
Outputs:
- solution: float32 [128, 128, 512], P('gx', 'gy', 'gz')
Inputs may be any that keep to these rules, and one draw needn't show every extreme that they name: `conductivity`: rows 0 to 2 are positive, rows 3 to 5 have magnitude at most 0.08, row 6 is at least 0.5.
All inputs are finite; a program needn't handle non-finite values.
Results may differ from a plain program's by a relative error of at most 0.0001.
Values sent between devices are 32-bit elements; how exact they have to be, the bound alone decides.
A program may use at most 128 MiB of HBM per device.

v0:
```python
import jax
import jax.numpy as jnp
from jax import lax
from jax.sharding import PartitionSpec as P

ITERS = 3


def with_halo(cells, sides, width):
    for axis, dim in sides:
        count = lax.axis_size(axis)
        ends = count - 1
        head = lax.slice_in_dim(cells, 0, width, axis=dim)
        tail = lax.slice_in_dim(cells, cells.shape[dim] - width, cells.shape[dim], axis=dim)
        cells = jnp.concatenate(
            [
                lax.ppermute(tail, axis, [(i, (i + 1) % count) for i in range(ends)]),
                cells,
                lax.ppermute(head, axis, [((i + 1) % count, i) for i in range(ends)]),
            ],
            axis=dim,
        )
    return cells


def neighbour_value(arr, shift_x, shift_y, shift_z, cell_grid):
    size_x, size_y, size_z = cell_grid
    return arr[
        ...,
        1 + shift_x : 1 + shift_x + size_x,
        1 + shift_y : 1 + shift_y + size_y,
        1 + shift_z : 1 + shift_z + size_z,
    ]


def stencil_apply(padded_value, padded_sigma, self_coefficient):
    cell_grid = self_coefficient.shape
    value_entry = neighbour_value(padded_value, 0, 0, 0, cell_grid)
    total_flux = self_coefficient * value_entry
    for axis in range(3):
        for sign in (-1, 1):
            stencil_offset = [0, 0, 0]
            stencil_offset[axis] = sign
            face_flux = 0.5 * (
                neighbour_value(padded_sigma[axis], 0, 0, 0, cell_grid)
                + neighbour_value(
                    padded_sigma[axis],
                    stencil_offset[0],
                    stencil_offset[1],
                    stencil_offset[2],
                    cell_grid,
                )
            )
            total_flux = total_flux + face_flux * (
                value_entry
                - neighbour_value(
                    padded_value, stencil_offset[0], stencil_offset[1], stencil_offset[2], cell_grid
                )
            )
    for first, second, comp in ((0, 1, 3), (0, 2, 4), (1, 2, 5)):
        for sign_a in (-1, 1):
            for sign_b in (-1, 1):
                stencil_offset = [0, 0, 0]
                stencil_offset[first] = sign_a
                stencil_offset[second] = sign_b
                cross_term = (
                    0.25
                    * sign_a
                    * sign_b
                    * (
                        neighbour_value(padded_sigma[comp], 0, 0, 0, cell_grid)
                        + neighbour_value(
                            padded_sigma[comp],
                            stencil_offset[0],
                            stencil_offset[1],
                            stencil_offset[2],
                            cell_grid,
                        )
                    )
                )
                total_flux = total_flux - cross_term * neighbour_value(
                    padded_value, stencil_offset[0], stencil_offset[1], stencil_offset[2], cell_grid
                )
    return total_flux


def diagonal_of(padded_sigma, self_coefficient):
    cell_grid = self_coefficient.shape
    total_flux = self_coefficient
    for axis in range(3):
        for sign in (-1, 1):
            stencil_offset = [0, 0, 0]
            stencil_offset[axis] = sign
            total_flux = total_flux + 0.5 * (
                neighbour_value(padded_sigma[axis], 0, 0, 0, cell_grid)
                + neighbour_value(
                    padded_sigma[axis],
                    stencil_offset[0],
                    stencil_offset[1],
                    stencil_offset[2],
                    cell_grid,
                )
            )
    return total_flux


def lookup(shifted, conductivity):
    total_flux = jnp.zeros((7,) + shifted.shape, jnp.float32)
    for label in range(conductivity.shape[1]):
        hit = (shifted == label + 1).astype(jnp.float32)
        total_flux = total_flux + hit[None] * conductivity[:, label][:, None, None, None]
    return total_flux


def apply_operator(field, padded_sigma, self_coefficient):
    field_pad = with_halo(field, (("gx", 0), ("gy", 1), ("gz", 2)), 1)
    return stencil_apply(field_pad, padded_sigma, self_coefficient)


def local(labels, conductivity, right_side):
    shifted = labels + 1
    own_table = lookup(shifted, conductivity)
    padded_sigma = with_halo(own_table[:6], (("gx", 1), ("gy", 2), ("gz", 3)), 1)
    self_coefficient = own_table[6]
    diag = diagonal_of(padded_sigma, self_coefficient)
    solution = jnp.zeros_like(right_side)
    residual = right_side
    precond = residual / diag
    applied = apply_operator(precond, padded_sigma, self_coefficient)
    gamma_old = jnp.float32(1.0)
    alpha_old = jnp.float32(1.0)
    direction = precond
    for step in range(ITERS):
        gamma, delta = lax.psum(
            (jnp.sum(residual * precond), jnp.sum(applied * precond)), ("gx", "gy", "gz")
        )
        if step + 1 < ITERS:
            scaled = applied / diag
            product = apply_operator(scaled, padded_sigma, self_coefficient)
        if step == 0:
            alpha = gamma / delta
            direction = precond
            along_z = product
            along_q = scaled
            along_s = applied
        else:
            ratio = gamma / gamma_old
            alpha = gamma / (delta - ratio * gamma / alpha_old)
            direction = precond + ratio * direction
            if step + 1 < ITERS:
                along_z = product + ratio * along_z
                along_q = scaled + ratio * along_q
                along_s = applied + ratio * along_s
        solution = solution + alpha * direction
        if step + 1 < ITERS:
            residual = residual - alpha * along_s
            precond = precond - alpha * along_q
            applied = applied - alpha * along_z
        gamma_old = gamma
        alpha_old = alpha
    return solution


def solution(mesh):
    return jax.shard_map(
        local,
        mesh=mesh,
        in_specs=(P("gx", "gy", "gz"), P(), P("gx", "gy", "gz")),
        out_specs=P("gx", "gy", "gz"),
        check_vma=False,
    )
```

profile of v0, /device:TPU:0, one launch (start us, length us, event | category | flops | bytes accessed | tf_op | source)
XLA Modules:
  0.0 398.3 jit_solution(9120328655755178801)
XLA Ops:
  1.3 2.3 compare_convert_fusion.7
  3.6 4.1 %multiply_add_fusion = f32[7,32,64,128]{3,2,1,0:T(8,128)S(1)} fusion(f32[7]{0:T(128)S(1)} %get-tuple-element.15, f32[32,64,128]{2,1,0:T(8,128)S(1)} %get-tuple-element.83, f32[7]{0:T(128)S(1)} %get-tuple-element.16, f32[32,64,128]{2,1,0:T(8,128)S(1)} %get-tuple-element.82, f32[7]{0:T(128)S(1)} %get-tuple-element.10, f32[32,64,128]{2,1,0:T(8,128)S(1)} %get-tuple-element.81, ...), kind=kLoop, calls=%fused_computation.2 | loop fusion | flops 27525120 | bytes 15728864 | tf_op jit(solution)/shard_map/add | solution.py:111
  7.8 4.9 %collective-permute-start = (f32[6,1,64,128]{3,2,1,0:T(8,128)S(1)}, f32[6,1,64,128]{3,2,1,0:T(8,128)S(1)}, u32[]{:S(2)}, u32[]{:S(2)}) collective-permute-start(f32[6,1,64,128]{3,2,1,0:T(8,128)S(1)} %get-tuple-element.42), channel_id=1, source_target_pairs={{0,8},{8,16},{16,24},{1,9},{9,17},{17,25},{2,10},{10,18},{18,26},{... | collective-permute-start | bytes 589832 | tf_op jit(solution)/shard_map/ppermute | solution.py:17
  16.8 6.2 %collective-permute-done.1 = f32[6,1,64,128]{3,2,1,0:T(8,128)S(1)} collective-permute-done((f32[6,1,64,128]{3,2,1,0:T(8,128)S(1)}, f32[6,1,64,128]{3,2,1,0:T(8,128)S(1)}, u32[]{:S(2)}, u32[]{:S(2)}) %collective-permute-start.1) | collective-permute-done | bytes 196640 | tf_op jit(solution)/shard_map/ppermute | solution.py:19
  27.6 3.6 pad_maximum_fusion.1
  31.2 12.6 %fusion.111 = (f32[6,34,66,1]{3,2,1,0:T(8,128)}, f32[6,34,66,1]{3,2,1,0:T(8,128)}) fusion(f32[6,34,66,128]{3,2,1,0:T(8,128)} %pad_maximum_fusion.1), kind=kLoop, calls=%fused_computation.239 | loop fusion | bytes 215424 | tf_op jit(solution)/shard_map/slice | solution.py:14
  43.8 5.1 %copy.16 = f32[6,34,66,1]{2,3,1,0:T(1,128)S(1)} copy(f32[6,34,66,1]{3,2,1,0:T(8,128)} %get-tuple-element.40) | data formatting | bytes 107712 | tf_op jit(solution)/shard_map/slice | solution.py:14
  48.9 3.5 collective-permute-start.4
  52.4 5.1 %copy.17 = f32[6,34,66,1]{2,3,1,0:T(1,128)S(1)} copy(f32[6,34,66,1]{3,2,1,0:T(8,128)} %get-tuple-element.41) | data formatting | bytes 107712 | tf_op jit(solution)/shard_map/slice | solution.py:13
  59.0 4.9 %copy.18 = f32[6,34,66,1]{3,2,1,0:T(8,128)} copy(f32[6,34,66,1]{2,3,1,0:T(1,128)S(1)} %collective-permute-done.4) | data formatting | bytes 107712 | tf_op jit(solution)/shard_map/ppermute | solution.py:17
  64.1 4.7 %copy.19 = f32[6,34,66,1]{3,2,1,0:T(8,128)} copy(f32[6,34,66,1]{2,3,1,0:T(1,128)S(1)} %collective-permute-done.5) | data formatting | bytes 107712 | tf_op jit(solution)/shard_map/ppermute | solution.py:19
  68.7 18.9 %pad_maximum_fusion = f32[6,34,66,130]{3,2,1,0:T(8,128)} fusion(f32[6,34,66,1]{3,2,1,0:T(8,128)} %copy.19, f32[6,34,1,128]{3,2,1,0:T(1,128)S(1)} %collective-permute-done.3, f32[6,1,64,128]{3,2,1,0:T(8,128)S(1)} %collective-permute-done.1, f32[6,32,64,128]{3,2,1,0:T(8,128)} %copy-done.9, f32[6,1,64,128]{3,2,1,0:T(8,128)S(1)} %collective-permute-done, ...), kind=kLoop, calls=%fused_computation | loop fusion | flops 10501920 | bytes 14002560 | tf_op jit(solution)/shard_map/concatenate | solution.py:15
  87.6 10.2 %slice_bitcast_fusion.2 = (f32[34,66,130]{2,1,0:T(8,128)S(1)}, f32[34,66,130]{2,1,0:T(8,128)}, f32[34,66,130]{2,1,0:T(8,128)}, f32[34,66,130]{2,1,0:T(8,128)}, f...) fusion(f32[6,34,66,130]{3,2,1,0:T(8,128)} %pad_maximum_fusion), kind=kLoop, calls=%fused_computation.5 | loop fusion | bytes 14002560 | tf_op jit(solution)/shard_map/squeeze | solution.py:71
  97.8 13.2 %fusion.104 = (f32[32,64,128]{2,1,0:T(8,128)S(1)}, f32[32,64,128]{2,1,0:T(8,128)}, f32[32,64,128]{2,1,0:T(8,128)}, f32[32,64,128]{2,1,0:T(8,128)}, f32[32,64,128...) fusion(f32[32,64,128]{2,1,0:T(8,128)} %param.5, ...), kind=kLoop, calls=%fused_computation.238 | loop fusion | flops 4980736 | bytes 19922944 | tf_op jit(solution)/shard_map/div | solution.py:128
  111.0 3.4 collective-permute-start.6
  116.0 4.2 %collective-permute-done.7 = f32[1,64,128]{2,1,0:T(8,128)S(1)} collective-permute-done((f32[1,64,128]{2,1,0:T(8,128)S(1)}, f32[1,64,128]{2,1,0:T(8,128)S(1)}, u32[]{:S(2)}, u32[]{:S(2)}) %collective-permute-start.7) | collective-permute-done | bytes 32800 | tf_op jit(solution)/shard_map/ppermute | solution.py:19
  127.2 2.4 copy.20
  129.6 2.4 copy.22
  133.3 5.6 %collective-permute-start.10 = (f32[34,66,1]{1,2,0:T(1,128)}, f32[34,66,1]{1,2,0:T(1,128)}, u32[]{:S(2)}, u32[]{:S(2)}) collective-permute-start(f32[34,66,1]{1,2,0:T(1,128)} %copy.20), channel_id=1, source_target_pairs={{0,1},{1,2},{2,3},{4,5},{5,6},{6,7},{8,9},{9,10},{10,11},{12,13},{... | collective-permute-start | bytes 26936 | tf_op jit(solution)/shard_map/ppermute | solution.py:17
  138.8 2.5 maximum_maximum_fusion.3
  141.3 2.3 copy.21
  143.6 2.4 copy.23
  146.0 3.8 maximum_maximum_fusion
  150.2 9.8 %multiply_reduce_fusion.3 = (f32[]{:T(128)}, f32[]{:T(128)}, f32[32,64,128]{2,1,0:T(8,128)S(1)}) fusion(f32[32,64,128]{2,1,0:T(8,128)S(1)} %get-tuple-element.26, f32[32,64,128]{2,1,0:T(8,128)} %param.5, f32[34,66,129]{2,1,0:T(8,128)S(1)} %get-tuple-element.57, f32[34,66,130]{2,1,0:T(8,128)S(1)} %copy-done, f32[34,66,129]{2,1,0:T(8,128)S(1)} %get-tuple-element.56, ...), kind=kLoop, calls=%fused_computation.206 | loop fusion | flops 19136512 | bytes 43057160 | tf_op jit(solution)/shard_map/reduce_sum | solution.py:135
  160.2 2.8 collective-permute-start.12
  164.6 4.2 %collective-permute-done.13 = f32[1,64,128]{2,1,0:T(8,128)S(1)} collective-permute-done((f32[1,64,128]{2,1,0:T(8,128)S(1)}, f32[1,64,128]{2,1,0:T(8,128)S(1)}, u32[]{:S(2)}, u32[]{:S(2)}) %collective-permute-start.13) | collective-permute-done | bytes 32800 | tf_op jit(solution)/shard_map/ppermute | solution.py:19
  172.6 40.9 %all-reduce.2 = (f32[]{:T(128)}, f32[]{:T(128)}) all-reduce(f32[]{:T(128)} %get-tuple-element.8, f32[]{:T(128)} %get-tuple-element.7), channel_id=1, replica_groups=mesh['gx'=4,'gy'=2,'gz'=4] {'gx','gy','gz'}, use_global_device_ids=true, to_apply=%region_1.0 | all-reduce | flops 2 | bytes 16 | tf_op jit(solution)/shard_map/psum | solution.py:134
  218.1 2.4 copy.24
  220.5 2.4 copy.26
  224.1 5.1 %collective-permute-start.16 = (f32[34,66,1]{1,2,0:T(1,128)}, f32[34,66,1]{1,2,0:T(1,128)}, u32[]{:S(2)}, u32[]{:S(2)}) collective-permute-start(f32[34,66,1]{1,2,0:T(1,128)} %copy.24), channel_id=1, source_target_pairs={{0,1},{1,2},{2,3},{4,5},{5,6},{6,7},{8,9},{9,10},{10,11},{12,13},{... | collective-permute-start | bytes 26936 | tf_op jit(solution)/shard_map/ppermute | solution.py:17
  229.3 3.3 maximum_maximum_fusion.4
  232.6 2.3 copy.25
  234.8 2.4 copy.27
  237.2 4.1 %maximum_maximum_fusion.1 = (f32[34,66,129]{2,1,0:T(8,128)S(1)}, f32[34,66,129]{2,1,0:T(8,128)S(1)}) fusion(f32[34,1,128]{2,1,0:T(1,128)} %collective-permute-done.15, f32[1,64,128]{2,1,0:T(8,128)} %copy-done.26, f32[32,64,128]{2,1,0:T(8,128)} %copy-done.6, f32[1,64,128]{2,1,0:T(8,128)} %copy-done.24, f32[34,1,128]{2,1,0:T(1,128)} %collective-permute-done.14, ...), kind=kLoop, calls=%fused_computation.11 | loop fusion | flops 2894760 | bytes 3482688 | tf_op jit(solution)/shard_map/concatenate | solution.py:15
  242.0 9.4 %fusion.101 = (f32[32,64,128]{2,1,0:T(8,128)S(1)}, f32[32,64,128]{2,1,0:T(8,128)S(1)}) fusion(f32[32,64,128]{2,1,0:T(8,128)S(1)} %copy-done.18, f32[32,64,128]{2,1,0:T(8,128)S(1)} %copy-done.11, f32[]{:T(128)S(6)} %div.31, f32[34,66,129]{2,1,0:T(8,128)S(1)} %get-tuple-element.55, f32[34,66,130]{2,1,0:T(8,128)S(1)} %copy-done.1, ...), kind=kLoop, calls=%fused_computation.217 | loop fusion | flops 18874368 | bytes 45154308 | tf_op jit(solution)/shard_map/div | solution.py:138
  252.2 4.8 %collective-permute-start.18 = (f32[1,64,128]{2,1,0:T(8,128)}, f32[1,64,128]{2,1,0:T(8,128)}, u32[]{:S(2)}, u32[]{:S(2)}) collective-permute-start(f32[1,64,128]{2,1,0:T(8,128)} %get-tuple-element.70), channel_id=1, source_target_pairs={{0,8},{8,16},{16,24},{1,9},{9,17},{17,25},{2,10},{10,18},{18,26},{... | collective-permute-start | bytes 98312 | tf_op jit(solution)/shard_map/ppermute | solution.py:17
  259.5 41.2 %all-reduce.1 = (f32[]{:T(128)}, f32[]{:T(128)}) all-reduce(f32[]{:T(128)} %get-tuple-element.6, f32[]{:T(128)} %get-tuple-element.5), channel_id=1, replica_groups=mesh['gx'=4,'gy'=2,'gz'=4] {'gx','gy','gz'}, use_global_device_ids=true, to_apply=%region_5.0 | all-reduce | flops 2 | bytes 16 | tf_op jit(solution)/shard_map/psum | solution.py:134
  309.1 3.8 multiply_reduce_fusion
  315.7 2.4 copy.28
  318.0 2.4 copy.30
  321.7 5.1 %collective-permute-start.22 = (f32[34,66,1]{1,2,0:T(1,128)}, f32[34,66,1]{1,2,0:T(1,128)}, u32[]{:S(2)}, u32[]{:S(2)}) collective-permute-start(f32[34,66,1]{1,2,0:T(1,128)} %copy.28), channel_id=1, source_target_pairs={{0,1},{1,2},{2,3},{4,5},{5,6},{6,7},{8,9},{9,10},{10,11},{12,13},{... | collective-permute-start | bytes 26936 | tf_op jit(solution)/shard_map/ppermute | solution.py:17
  326.8 3.3 maximum_maximum_fusion.5
  330.1 2.3 copy.29
  332.4 2.4 copy.31
  334.8 4.1 %maximum_maximum_fusion.2 = (f32[34,66,129]{2,1,0:T(8,128)S(1)}, f32[34,66,129]{2,1,0:T(8,128)S(1)}) fusion(f32[34,1,128]{2,1,0:T(1,128)} %copy-done.34, f32[1,64,128]{2,1,0:T(8,128)} %collective-permute-done.19, f32[32,64,128]{2,1,0:T(8,128)} %copy-done.14, f32[1,64,128]{2,1,0:T(8,128)} %collective-permute-done.18, f32[34,1,128]{2,1,0:T(1,128)} %copy-done.32, ...), kind=kLoop, calls=%fused_computation.13 | loop fusion | flops 2894760 | bytes 3482688 | tf_op jit(solution)/shard_map/concatenate | solution.py:15
  339.6 10.8 %fusion.5 = f32[]{:T(128)} fusion(f32[34,66,129]{2,1,0:T(8,128)S(1)} %get-tuple-element.53, f32[34,66,129]{2,1,0:T(8,128)S(1)} %get-tuple-element.52, f32[34,65,128]{2,1,0:T(8,128)} %get-tuple-element.59, f32[34,65,128]{2,1,0:T(8,128)} %get-tuple-element.58, f32[32,64,128]{2,1,0:T(8,128)} %get-tuple-element.33, f32[32,64,128]{2,1,0:T(8,128)S(1)} %copy-done.16, ...), kind=kLoop, calls=%fused_computation.30 | loop fusion | flops 22020096 | bytes 46202896 | tf_op jit(solution)/shard_map/reduce_sum | solution.py:135
  350.3 40.4 %all-reduce = (f32[]{:T(128)}, f32[]{:T(128)}) all-reduce(f32[]{:T(128)} %multiply_reduce_fusion, f32[]{:T(128)} %fusion.5), channel_id=1, replica_groups=mesh['gx'=4,'gy'=2,'gz'=4] {'gx','gy','gz'}, use_global_device_ids=true, to_apply=%region_9.0 | all-reduce | flops 2 | bytes 16 | tf_op jit(solution)/shard_map/psum | solution.py:134
  394.5 3.8 multiply_add_fusion.1
  (127 shorter events, 44.8 us)
Async XLA Ops:
  7.7 7.4 %copy-start.13 = (f32[7,32,64,128]{3,2,1,0:T(8,128)}, f32[7,32,64,128]{3,2,1,0:T(8,128)S(1)}, u32[]{:S(2)}) copy-start(f32[7,32,64,128]{3,2,1,0:T(8,128)S(1)} %multiply_add_fusion) | copy-start | bytes 22020100
  7.8 9.0 %collective-permute-start = (f32[6,1,64,128]{3,2,1,0:T(8,128)S(1)}, f32[6,1,64,128]{3,2,1,0:T(8,128)S(1)}, u32[]{:S(2)}, u32[]{:S(2)}) collective-permute-start(f32[6,1,64,128]{3,2,1,0:T(8,128)S(1)} %get-tuple-element.42), channel_id=1, source_target_pairs={{0,8},{8,16},{16,24},{1,9},{9,17},{17,25},{2,10},{10,18},{18,26},{... | collective-permute-start | bytes 589832 | tf_op jit(solution)/shard_map/ppermute | solution.py:17
  12.7 10.3 %collective-permute-start.1 = (f32[6,1,64,128]{3,2,1,0:T(8,128)S(1)}, f32[6,1,64,128]{3,2,1,0:T(8,128)S(1)}, u32[]{:S(2)}, u32[]{:S(2)}) collective-permute-start(f32[6,1,64,128]{3,2,1,0:T(8,128)S(1)} %get-tuple-element.43), channel_id=1, source_target_pairs={{8,0},{16,8},{24,16},{9,1},{17,9},{25,17},{10,2},{18,10},{26,18},{... | collective-permute-start | bytes 589832 | tf_op jit(solution)/shard_map/ppermute | solution.py:19
  15.1 12.5 %copy-start.9 = (f32[6,32,64,128]{3,2,1,0:T(8,128)}, f32[6,32,64,128]{3,2,1,0:T(8,128)S(1)}, u32[]{:S(2)}) copy-start(f32[6,32,64,128]{3,2,1,0:T(8,128)S(1)} %slice.740) | copy-start | bytes 18874372
  23.1 2.6 collective-permute-start.2
  24.4 3.2 collective-permute-start.3
  48.9 10.1 %collective-permute-start.4 = (f32[6,34,66,1]{2,3,1,0:T(1,128)S(1)}, f32[6,34,66,1]{2,3,1,0:T(1,128)S(1)}, u32[]{:S(2)}, u32[]{:S(2)}) collective-permute-start(f32[6,34,66,1]{2,3,1,0:T(1,128)S(1)} %copy.16), channel_id=1, source_target_pairs={{0,1},{1,2},{2,3},{4,5},{5,6},{6,7},{8,9},{9,10},{10,11},{12,13},{... | collective-permute-start | bytes 161576 | tf_op jit(solution)/shard_map/ppermute | solution.py:17
  57.5 6.6 %collective-permute-start.5 = (f32[6,34,66,1]{2,3,1,0:T(1,128)S(1)}, f32[6,34,66,1]{2,3,1,0:T(1,128)S(1)}, u32[]{:S(2)}, u32[]{:S(2)}) collective-permute-start(f32[6,34,66,1]{2,3,1,0:T(1,128)S(1)} %copy.17), channel_id=1, source_target_pairs={{1,0},{2,1},{3,2},{5,4},{6,5},{7,6},{9,8},{10,9},{11,10},{13,12},{... | collective-permute-start | bytes 161576 | tf_op jit(solution)/shard_map/ppermute | solution.py:19
  111.0 5.0 %collective-permute-start.6 = (f32[1,64,128]{2,1,0:T(8,128)S(1)}, f32[1,64,128]{2,1,0:T(8,128)S(1)}, u32[]{:S(2)}, u32[]{:S(2)}) collective-permute-start(f32[1,64,128]{2,1,0:T(8,128)S(1)} %get-tuple-element.74), channel_id=1, source_target_pairs={{0,8},{8,16},{16,24},{1,9},{9,17},{17,25},{2,10},{10,18},{18,26},{... | collective-permute-start | bytes 98312 | tf_op jit(solution)/shard_map/ppermute | solution.py:17
  114.4 5.8 %collective-permute-start.7 = (f32[1,64,128]{2,1,0:T(8,128)S(1)}, f32[1,64,128]{2,1,0:T(8,128)S(1)}, u32[]{:S(2)}, u32[]{:S(2)}) collective-permute-start(f32[1,64,128]{2,1,0:T(8,128)S(1)} %get-tuple-element.75), channel_id=1, source_target_pairs={{8,0},{16,8},{24,16},{9,1},{17,9},{25,17},{10,2},{18,10},{26,18},{... | collective-permute-start | bytes 98312 | tf_op jit(solution)/shard_map/ppermute | solution.py:19
  116.0 8.6 %copy-start.28 = (f32[1,64,128]{2,1,0:T(8,128)}, f32[1,64,128]{2,1,0:T(8,128)S(1)}, u32[]{:S(2)}) copy-start(f32[1,64,128]{2,1,0:T(8,128)S(1)} %collective-permute-done.6) | copy-start | bytes 98308
  120.2 4.4 %copy-start.30 = (f32[1,64,128]{2,1,0:T(8,128)}, f32[1,64,128]{2,1,0:T(8,128)S(1)}, u32[]{:S(2)}) copy-start(f32[1,64,128]{2,1,0:T(8,128)S(1)} %collective-permute-done.7) | copy-start | bytes 98308
  120.3 2.6 collective-permute-start.8
  121.6 3.1 collective-permute-start.9
  132.0 11.6 %collective-permute-start.11 = (f32[34,66,1]{1,2,0:T(1,128)}, f32[34,66,1]{1,2,0:T(1,128)}, u32[]{:S(2)}, u32[]{:S(2)}) collective-permute-start(f32[34,66,1]{1,2,0:T(1,128)} %copy.22), channel_id=1, source_target_pairs={{1,0},{2,1},{3,2},{5,4},{6,5},{7,6},{9,8},{10,9},{11,10},{13,12},{... | collective-permute-start | bytes 26936 | tf_op jit(solution)/shard_map/ppermute | solution.py:19
  133.3 8.0 %collective-permute-start.10 = (f32[34,66,1]{1,2,0:T(1,128)}, f32[34,66,1]{1,2,0:T(1,128)}, u32[]{:S(2)}, u32[]{:S(2)}) collective-permute-start(f32[34,66,1]{1,2,0:T(1,128)} %copy.20), channel_id=1, source_target_pairs={{0,1},{1,2},{2,3},{4,5},{5,6},{6,7},{8,9},{9,10},{10,11},{12,13},{... | collective-permute-start | bytes 26936 | tf_op jit(solution)/shard_map/ppermute | solution.py:17
  146.0 4.2 %copy-start.22 = (f32[32,64,128]{2,1,0:T(8,128)S(1)}, f32[32,64,128]{2,1,0:T(8,128)}, u32[]{:S(2)}) copy-start(f32[32,64,128]{2,1,0:T(8,128)} %get-tuple-element.30) | copy-start | bytes 3145732
  146.0 4.2 %copy-start.29 = (f32[1,64,128]{2,1,0:T(8,128)S(1)}, f32[1,64,128]{2,1,0:T(8,128)}, u32[]{:S(2)}) copy-start(f32[1,64,128]{2,1,0:T(8,128)} %copy-done.28) | copy-start | bytes 98308
  146.0 4.2 %copy-start.31 = (f32[1,64,128]{2,1,0:T(8,128)S(1)}, f32[1,64,128]{2,1,0:T(8,128)}, u32[]{:S(2)}) copy-start(f32[1,64,128]{2,1,0:T(8,128)} %copy-done.30) | copy-start | bytes 98308
  150.2 9.8 %copy-start.17 = (f32[32,64,128]{2,1,0:T(8,128)S(1)}, f32[32,64,128]{2,1,0:T(8,128)}, u32[]{:S(2)}) copy-start(f32[32,64,128]{2,1,0:T(8,128)} %get-tuple-element.27) | copy-start | bytes 3145732
  160.0 9.5 %copy-start.10 = (f32[32,64,128]{2,1,0:T(8,128)}, f32[32,64,128]{2,1,0:T(8,128)S(1)}, u32[]{:S(2)}) copy-start(f32[32,64,128]{2,1,0:T(8,128)S(1)} %get-tuple-element.25) | copy-start | bytes 3145732
  160.1 8.7 %copy-start.6 = (f32[32,64,128]{2,1,0:T(8,128)}, f32[32,64,128]{2,1,0:T(8,128)S(1)}, u32[]{:S(2)}) copy-start(f32[32,64,128]{2,1,0:T(8,128)S(1)} %div.32) | copy-start | bytes 3145732
  160.2 4.4 %collective-permute-start.12 = (f32[1,64,128]{2,1,0:T(8,128)S(1)}, f32[1,64,128]{2,1,0:T(8,128)S(1)}, u32[]{:S(2)}, u32[]{:S(2)}) collective-permute-start(f32[1,64,128]{2,1,0:T(8,128)S(1)} %get-tuple-element.72), channel_id=1, source_target_pairs={{0,8},{8,16},{16,24},{1,9},{9,17},{17,25},{2,10},{10,18},{18,26},{... | collective-permute-start | bytes 98312 | tf_op jit(solution)/shard_map/ppermute | solution.py:17
  163.0 5.8 %collective-permute-start.13 = (f32[1,64,128]{2,1,0:T(8,128)S(1)}, f32[1,64,128]{2,1,0:T(8,128)S(1)}, u32[]{:S(2)}, u32[]{:S(2)}) collective-permute-start(f32[1,64,128]{2,1,0:T(8,128)S(1)} %get-tuple-element.73), channel_id=1, source_target_pairs={{8,0},{16,8},{24,16},{9,1},{17,9},{25,17},{10,2},{18,10},{26,18},{... | collective-permute-start | bytes 98312 | tf_op jit(solution)/shard_map/ppermute | solution.py:19
  164.6 4.9 %copy-start.24 = (f32[1,64,128]{2,1,0:T(8,128)}, f32[1,64,128]{2,1,0:T(8,128)S(1)}, u32[]{:S(2)}) copy-start(f32[1,64,128]{2,1,0:T(8,128)S(1)} %collective-permute-done.12) | copy-start | bytes 98308
  169.4 45.5 %collective-permute-start.14 = (f32[34,1,128]{2,1,0:T(1,128)}, f32[34,1,128]{2,1,0:T(1,128)}, u32[]{:S(2)}, u32[]{:S(2)}) collective-permute-start(f32[34,1,128]{2,1,0:T(1,128)} %get-tuple-element.64), channel_id=1, source_target_pairs={{0,4},{1,5},{2,6},{3,7},{8,12},{9,13},{10,14},{11,15},{16,20},{17,... | collective-permute-start | bytes 52232 | tf_op jit(solution)/shard_map/ppermute | solution.py:17
  171.3 43.6 %collective-permute-start.15 = (f32[34,1,128]{2,1,0:T(1,128)}, f32[34,1,128]{2,1,0:T(1,128)}, u32[]{:S(2)}, u32[]{:S(2)}) collective-permute-start(f32[34,1,128]{2,1,0:T(1,128)} %get-tuple-element.65), channel_id=1, source_target_pairs={{4,0},{5,1},{6,2},{7,3},{12,8},{13,9},{14,10},{15,11},{20,16},{21,... | collective-permute-start | bytes 52232 | tf_op jit(solution)/shard_map/ppermute | solution.py:19
  222.9 12.0 %collective-permute-start.17 = (f32[34,66,1]{1,2,0:T(1,128)}, f32[34,66,1]{1,2,0:T(1,128)}, u32[]{:S(2)}, u32[]{:S(2)}) collective-permute-start(f32[34,66,1]{1,2,0:T(1,128)} %copy.26), channel_id=1, source_target_pairs={{1,0},{2,1},{3,2},{5,4},{6,5},{7,6},{9,8},{10,9},{11,10},{13,12},{... | collective-permute-start | bytes 26936 | tf_op jit(solution)/shard_map/ppermute | solution.py:19
  224.1 8.4 %collective-permute-start.16 = (f32[34,66,1]{1,2,0:T(1,128)}, f32[34,66,1]{1,2,0:T(1,128)}, u32[]{:S(2)}, u32[]{:S(2)}) collective-permute-start(f32[34,66,1]{1,2,0:T(1,128)} %copy.24), channel_id=1, source_target_pairs={{0,1},{1,2},{2,3},{4,5},{5,6},{6,7},{8,9},{9,10},{10,11},{12,13},{... | collective-permute-start | bytes 26936 | tf_op jit(solution)/shard_map/ppermute | solution.py:17
  237.2 4.1 %copy-start.4 = (f32[34,66,130]{2,1,0:T(8,128)S(1)}, f32[34,66,130]{2,1,0:T(8,128)}, u32[]{:S(2)}) copy-start(f32[34,66,130]{2,1,0:T(8,128)} %get-tuple-element.36) | copy-start | bytes 3500644
  237.2 4.2 %copy-start.7 = (f32[32,64,128]{2,1,0:T(8,128)S(1)}, f32[32,64,128]{2,1,0:T(8,128)}, u32[]{:S(2)}) copy-start(f32[32,64,128]{2,1,0:T(8,128)} %copy-done.6) | copy-start | bytes 3145732
  237.2 4.5 %copy-start.11 = (f32[32,64,128]{2,1,0:T(8,128)S(1)}, f32[32,64,128]{2,1,0:T(8,128)}, u32[]{:S(2)}) copy-start(f32[32,64,128]{2,1,0:T(8,128)} %copy-done.10) | copy-start | bytes 3145732
  237.2 4.8 %copy-start.18 = (f32[32,64,128]{2,1,0:T(8,128)S(1)}, f32[32,64,128]{2,1,0:T(8,128)}, u32[]{:S(2)}) copy-start(f32[32,64,128]{2,1,0:T(8,128)} %get-tuple-element.27) | copy-start | bytes 3145732
  237.2 4.8 %copy-start.25 = (f32[1,64,128]{2,1,0:T(8,128)S(1)}, f32[1,64,128]{2,1,0:T(8,128)}, u32[]{:S(2)}) copy-start(f32[1,64,128]{2,1,0:T(8,128)} %copy-done.24) | copy-start | bytes 98308
  237.2 4.8 %copy-start.27 = (f32[1,64,128]{2,1,0:T(8,128)S(1)}, f32[1,64,128]{2,1,0:T(8,128)}, u32[]{:S(2)}) copy-start(f32[1,64,128]{2,1,0:T(8,128)} %copy-done.26) | copy-start | bytes 98308
  242.0 16.2 %copy-start.23 = (f32[32,64,128]{2,1,0:T(8,128)S(1)}, f32[32,64,128]{2,1,0:T(8,128)}, u32[]{:S(2)}) copy-start(f32[32,64,128]{2,1,0:T(8,128)} %param.5) | copy-start | bytes 3145732
  251.5 8.0 %copy-start.14 = (f32[32,64,128]{2,1,0:T(8,128)}, f32[32,64,128]{2,1,0:T(8,128)S(1)}, u32[]{:S(2)}) copy-start(f32[32,64,128]{2,1,0:T(8,128)S(1)} %get-tuple-element.23) | copy-start | bytes 3145732
  251.5 8.0 %copy-start.19 = (f32[32,64,128]{2,1,0:T(8,128)}, f32[32,64,128]{2,1,0:T(8,128)S(1)}, u32[]{:S(2)}) copy-start(f32[32,64,128]{2,1,0:T(8,128)S(1)} %get-tuple-element.24) | copy-start | bytes 3145732
  252.2 52.9 %collective-permute-start.18 = (f32[1,64,128]{2,1,0:T(8,128)}, f32[1,64,128]{2,1,0:T(8,128)}, u32[]{:S(2)}, u32[]{:S(2)}) collective-permute-start(f32[1,64,128]{2,1,0:T(8,128)} %get-tuple-element.70), channel_id=1, source_target_pairs={{0,8},{8,16},{16,24},{1,9},{9,17},{17,25},{2,10},{10,18},{18,26},{... | collective-permute-start | bytes 98312 | tf_op jit(solution)/shard_map/ppermute | solution.py:17
  257.0 48.2 %collective-permute-start.19 = (f32[1,64,128]{2,1,0:T(8,128)}, f32[1,64,128]{2,1,0:T(8,128)}, u32[]{:S(2)}, u32[]{:S(2)}) collective-permute-start(f32[1,64,128]{2,1,0:T(8,128)} %get-tuple-element.71), channel_id=1, source_target_pairs={{8,0},{16,8},{24,16},{9,1},{17,9},{25,17},{10,2},{18,10},{26,18},{... | collective-permute-start | bytes 98312 | tf_op jit(solution)/shard_map/ppermute | solution.py:19
  306.1 6.8 %collective-permute-start.20 = (f32[34,1,128]{2,1,0:T(1,128)S(1)}, f32[34,1,128]{2,1,0:T(1,128)S(1)}, u32[]{:S(2)}, u32[]{:S(2)}) collective-permute-start(f32[34,1,128]{2,1,0:T(1,128)S(1)} %get-tuple-element.60), channel_id=1, source_target_pairs={{0,4},{1,5},{2,6},{3,7},{8,12},{9,13},{10,14},{11,15},{16,20},{17,... | collective-permute-start | bytes 52232 | tf_op jit(solution)/shard_map/ppermute | solution.py:17
  307.4 5.5 %copy-start.15 = (f32[32,64,128]{2,1,0:T(8,128)S(1)}, f32[32,64,128]{2,1,0:T(8,128)}, u32[]{:S(2)}) copy-start(f32[32,64,128]{2,1,0:T(8,128)} %copy-done.14) | copy-start | bytes 3145732
  307.4 5.5 %collective-permute-start.21 = (f32[34,1,128]{2,1,0:T(1,128)S(1)}, f32[34,1,128]{2,1,0:T(1,128)S(1)}, u32[]{:S(2)}, u32[]{:S(2)}) collective-permute-start(f32[34,1,128]{2,1,0:T(1,128)S(1)} %get-tuple-element.61), channel_id=1, source_target_pairs={{4,0},{5,1},{6,2},{7,3},{12,8},{13,9},{14,10},{15,11},{20,16},{21,... | collective-permute-start | bytes 52232 | tf_op jit(solution)/shard_map/ppermute | solution.py:19
  320.4 12.0 %collective-permute-start.23 = (f32[34,66,1]{1,2,0:T(1,128)}, f32[34,66,1]{1,2,0:T(1,128)}, u32[]{:S(2)}, u32[]{:S(2)}) collective-permute-start(f32[34,66,1]{1,2,0:T(1,128)} %copy.30), channel_id=1, source_target_pairs={{1,0},{2,1},{3,2},{5,4},{6,5},{7,6},{9,8},{10,9},{11,10},{13,12},{... | collective-permute-start | bytes 26936 | tf_op jit(solution)/shard_map/ppermute | solution.py:19
  321.7 8.4 %collective-permute-start.22 = (f32[34,66,1]{1,2,0:T(1,128)}, f32[34,66,1]{1,2,0:T(1,128)}, u32[]{:S(2)}, u32[]{:S(2)}) collective-permute-start(f32[34,66,1]{1,2,0:T(1,128)} %copy.28), channel_id=1, source_target_pairs={{0,1},{1,2},{2,3},{4,5},{5,6},{6,7},{8,9},{9,10},{10,11},{12,13},{... | collective-permute-start | bytes 26936 | tf_op jit(solution)/shard_map/ppermute | solution.py:17
  334.7 4.2 %copy-start.8 = (f32[32,64,128]{2,1,0:T(8,128)S(1)}, f32[32,64,128]{2,1,0:T(8,128)}, u32[]{:S(2)}) copy-start(f32[32,64,128]{2,1,0:T(8,128)} %copy-done.6) | copy-start | bytes 3145732
  334.7 4.5 %copy-start.12 = (f32[32,64,128]{2,1,0:T(8,128)S(1)}, f32[32,64,128]{2,1,0:T(8,128)}, u32[]{:S(2)}) copy-start(f32[32,64,128]{2,1,0:T(8,128)} %copy-done.10) | copy-start | bytes 3145732
  334.8 4.8 %copy-start.16 = (f32[32,64,128]{2,1,0:T(8,128)S(1)}, f32[32,64,128]{2,1,0:T(8,128)}, u32[]{:S(2)}) copy-start(f32[32,64,128]{2,1,0:T(8,128)} %copy-done.14) | copy-start | bytes 3145732
  (12 other events, 38.1 us)
where the time goes:
time: 400 us; the launch traced here: 398 us
  blocking collectives  123 us (31%)
  other arithmetic  106 us (26%)
  local copies, waits for them, and re-layouts  81.7 us (20%)
  starting transfers between devices  57 us (14%)
  waiting for transfers between devices  20.8 us (5%)
  between operations  10.1 us (3%)
    psum x3, blocking collectives, local(): lax.psum((jnp.sum(residual * precond), jnp.sum(applied * precond)), ('gx'...  123 us
    concatenate x11, other arithmetic, with_halo(): jnp.concatenate([lax.ppermute(tail, axis, [(i, (i + 1) % count) for i in...  45.8 us
    ppermute x12, starting transfers between devices, with_halo(): lax.ppermute(tail, axis, [(i, (i + 1) % count) for i in range(ends)])  41 us
    slice x12, local copies, waits for them, and re-layouts, with_halo(): lax.slice_in_dim(cells, cells.shape[dim] - width, cells.shape[dim], axis=...  31 us
    reduce_sum x3, other arithmetic, local(): jnp.sum(applied * precond)  21.8 us
    ppermute x12, waiting for transfers between devices, with_halo(): lax.ppermute(head, axis, [((i + 1) % count, i) for i in range(ends)])  18.5 us
    ppermute x12, starting transfers between devices, with_halo(): lax.ppermute(head, axis, [((i + 1) % count, i) for i in range(ends)])  16 us
    div x1, other arithmetic, local(): precond = residual / diag  13.2 us
  transfers between devices with their start and end apart: 24, of which 9 were waited for; matrix products, arithmetic and copies ran while one was open for 8% of the time, Pallas kernels for 0%

commit v1 on v0

--- a/solution.py
+++ b/solution.py
@@ -131,9 +131,10 @@
     alpha_old = jnp.float32(1.0)
     direction = precond
     for step in range(ITERS):
-        gamma, delta = lax.psum(
-            (jnp.sum(residual * precond), jnp.sum(applied * precond)), ("gx", "gy", "gz")
+        launch_fields = lambda panel: lax.psum(
+            lax.psum(panel, axis_name=("gy", "gz")), axis_name="gx"
         )
+        gamma, delta = launch_fields((jnp.sum(residual * precond), jnp.sum(applied * precond)))
         if step + 1 < ITERS:
             scaled = applied / diag
             product = apply_operator(scaled, padded_sigma, self_coefficient)

time: 400 us -> 356 us (0.89)
  blocking collectives: 123 us -> 80.3 us
    psum x3 -> x6, blocking collectives: 123 us -> 80.3 us  [the longest x3 50.3 us: local(): lax.psum(panel, axis_name=('gy', 'gz'))]
  transfers between devices with their start and end apart: 24 -> 24, of which waited for: 9 -> 9; matrix products, arithmetic and copies ran while one was open for 8% -> 9% of each run, Pallas kernels for 0% -> 0%
where the time goes in v1:
time: 356 us; the launch traced here: 354 us
  other arithmetic  106 us (30%)
  local copies, waits for them, and re-layouts  81.5 us (23%)
  blocking collectives  80.3 us (23%)
  starting transfers between devices  55.5 us (16%)
  waiting for transfers between devices  20.8 us (6%)
  between operations  9.92 us (3%)
    psum x3, blocking collectives, local(): lax.psum(panel, axis_name=('gy', 'gz'))  50.3 us
    concatenate x11, other arithmetic, with_halo(): jnp.concatenate([lax.ppermute(tail, axis, [(i, (i + 1) % count) for i in...  46 us
    ppermute x12, starting transfers between devices, with_halo(): lax.ppermute(tail, axis, [(i, (i + 1) % count) for i in range(ends)])  39.7 us
    slice x12, local copies, waits for them, and re-layouts, with_halo(): lax.slice_in_dim(cells, cells.shape[dim] - width, cells.shape[dim], axis=...  31 us
    psum x3, blocking collectives, local(): lax.psum(lax.psum(panel, axis_name=('gy', 'gz')), axis_name='gx')  30 us
    reduce_sum x3, other arithmetic, local(): jnp.sum(applied * precond)  21.8 us
    ppermute x12, waiting for transfers between devices, with_halo(): lax.ppermute(head, axis, [((i + 1) % count, i) for i in range(ends)])  18.5 us
    ppermute x12, starting transfers between devices, with_halo(): lax.ppermute(head, axis, [((i + 1) % count, i) for i in range(ends)])  15.8 us
  transfers between devices with their start and end apart: 24, of which 9 were waited for; matrix products, arithmetic and copies ran while one was open for 9% of the time, Pallas kernels for 0%

profile of v1, /device:TPU:0, one launch (start us, length us, event | category | flops | bytes accessed | tf_op | source)
XLA Modules:
  0.0 354.1 jit_solution(11190124885855075967)
XLA Ops:
  3.3 4.1 %multiply_add_fusion = f32[7,32,64,128]{3,2,1,0:T(8,128)S(1)} fusion(f32[7]{0:T(128)S(1)} %get-tuple-element.15, f32[32,64,128]{2,1,0:T(8,128)S(1)} %get-tuple-element.89, f32[7]{0:T(128)S(1)} %get-tuple-element.16, f32[32,64,128]{2,1,0:T(8,128)S(1)} %get-tuple-element.88, f32[7]{0:T(128)S(1)} %get-tuple-element.10, f32[32,64,128]{2,1,0:T(8,128)S(1)} %get-tuple-element.87, ...), kind=kLoop, calls=%fused_computation.2 | loop fusion | flops 27525120 | bytes 15728864 | tf_op jit(solution)/shard_map/add | solution.py:111
  7.5 4.9 %collective-permute-start = (f32[6,1,64,128]{3,2,1,0:T(8,128)S(1)}, f32[6,1,64,128]{3,2,1,0:T(8,128)S(1)}, u32[]{:S(2)}, u32[]{:S(2)}) collective-permute-start(f32[6,1,64,128]{3,2,1,0:T(8,128)S(1)} %get-tuple-element.48), channel_id=1, source_target_pairs={{0,8},{8,16},{16,24},{1,9},{9,17},{17,25},{2,10},{10,18},{18,26},{... | collective-permute-start | bytes 589832 | tf_op jit(solution)/shard_map/ppermute | solution.py:17
  16.5 6.2 %collective-permute-done.1 = f32[6,1,64,128]{3,2,1,0:T(8,128)S(1)} collective-permute-done((f32[6,1,64,128]{3,2,1,0:T(8,128)S(1)}, f32[6,1,64,128]{3,2,1,0:T(8,128)S(1)}, u32[]{:S(2)}, u32[]{:S(2)}) %collective-permute-start.1) | collective-permute-done | bytes 196640 | tf_op jit(solution)/shard_map/ppermute | solution.py:19
  27.3 3.6 %pad_maximum_fusion.1 = f32[6,34,66,128]{3,2,1,0:T(8,128)} fusion(f32[6,34,1,128]{3,2,1,0:T(1,128)S(1)} %collective-permute-done.3, f32[6,1,64,128]{3,2,1,0:T(8,128)S(1)} %collective-permute-done.1, f32[6,32,64,128]{3,2,1,0:T(8,128)S(1)} %slice.740, f32[6,1,64,128]{3,2,1,0:T(8,128)S(1)} %collective-permute-done, f32[6,34,1,128]{3,2,1,0:T(1,128)S(1)} %collective-permute-done.2), kind=kLoop, calls=%fused_computation.1 | loop fusion | flops 6893568 | bytes 13787136 | tf_op jit(solution)/shard_map/concatenate | solution.py:15
  30.9 12.6 %fusion.111 = (f32[6,34,66,1]{3,2,1,0:T(8,128)}, f32[6,34,66,1]{3,2,1,0:T(8,128)}) fusion(f32[6,34,66,128]{3,2,1,0:T(8,128)} %pad_maximum_fusion.1), kind=kLoop, calls=%fused_computation.239 | loop fusion | bytes 215424 | tf_op jit(solution)/shard_map/slice | solution.py:14
  43.4 5.1 %copy.16 = f32[6,34,66,1]{2,3,1,0:T(1,128)S(1)} copy(f32[6,34,66,1]{3,2,1,0:T(8,128)} %get-tuple-element.46) | data formatting | bytes 107712 | tf_op jit(solution)/shard_map/slice | solution.py:14
  48.6 3.5 collective-permute-start.4
  52.1 5.1 %copy.17 = f32[6,34,66,1]{2,3,1,0:T(1,128)S(1)} copy(f32[6,34,66,1]{3,2,1,0:T(8,128)} %get-tuple-element.47) | data formatting | bytes 107712 | tf_op jit(solution)/shard_map/slice | solution.py:13
  58.7 4.9 %copy.18 = f32[6,34,66,1]{3,2,1,0:T(8,128)} copy(f32[6,34,66,1]{2,3,1,0:T(1,128)S(1)} %collective-permute-done.4) | data formatting | bytes 107712 | tf_op jit(solution)/shard_map/ppermute | solution.py:17
  63.8 4.6 %copy.19 = f32[6,34,66,1]{3,2,1,0:T(8,128)} copy(f32[6,34,66,1]{2,3,1,0:T(1,128)S(1)} %collective-permute-done.5) | data formatting | bytes 107712 | tf_op jit(solution)/shard_map/ppermute | solution.py:19
  68.4 19.0 %pad_maximum_fusion = f32[6,34,66,130]{3,2,1,0:T(8,128)} fusion(f32[6,34,66,1]{3,2,1,0:T(8,128)} %copy.19, f32[6,34,1,128]{3,2,1,0:T(1,128)S(1)} %collective-permute-done.3, f32[6,1,64,128]{3,2,1,0:T(8,128)S(1)} %collective-permute-done.1, f32[6,32,64,128]{3,2,1,0:T(8,128)} %copy-done.9, f32[6,1,64,128]{3,2,1,0:T(8,128)S(1)} %collective-permute-done, ...), kind=kLoop, calls=%fused_computation | loop fusion | flops 10501920 | bytes 14002560 | tf_op jit(solution)/shard_map/concatenate | solution.py:15
  87.4 10.2 %slice_bitcast_fusion.2 = (f32[34,66,130]{2,1,0:T(8,128)S(1)}, f32[34,66,130]{2,1,0:T(8,128)}, f32[34,66,130]{2,1,0:T(8,128)}, f32[34,66,130]{2,1,0:T(8,128)}, f...) fusion(f32[6,34,66,130]{3,2,1,0:T(8,128)} %pad_maximum_fusion), kind=kLoop, calls=%fused_computation.5 | loop fusion | bytes 14002560 | tf_op jit(solution)/shard_map/squeeze | solution.py:71
  97.5 13.1 %fusion.104 = (f32[32,64,128]{2,1,0:T(8,128)S(1)}, f32[32,64,128]{2,1,0:T(8,128)}, f32[32,64,128]{2,1,0:T(8,128)}, f32[32,64,128]{2,1,0:T(8,128)}, f32[32,64,128...) fusion(f32[32,64,128]{2,1,0:T(8,128)} %param.5, ...), kind=kLoop, calls=%fused_computation.238 | loop fusion | flops 4980736 | bytes 19922944 | tf_op jit(solution)/shard_map/div | solution.py:128
  110.7 3.4 collective-permute-start.6
  115.7 4.2 %collective-permute-done.7 = f32[1,64,128]{2,1,0:T(8,128)S(1)} collective-permute-done((f32[1,64,128]{2,1,0:T(8,128)S(1)}, f32[1,64,128]{2,1,0:T(8,128)S(1)}, u32[]{:S(2)}, u32[]{:S(2)}) %collective-permute-start.7) | collective-permute-done | bytes 32800 | tf_op jit(solution)/shard_map/ppermute | solution.py:19
  126.9 2.4 copy.20
  129.3 2.4 copy.22
  132.9 5.5 %collective-permute-start.10 = (f32[34,66,1]{1,2,0:T(1,128)}, f32[34,66,1]{1,2,0:T(1,128)}, u32[]{:S(2)}, u32[]{:S(2)}) collective-permute-start(f32[34,66,1]{1,2,0:T(1,128)} %copy.20), channel_id=1, source_target_pairs={{0,1},{1,2},{2,3},{4,5},{5,6},{6,7},{8,9},{9,10},{10,11},{12,13},{... | collective-permute-start | bytes 26936 | tf_op jit(solution)/shard_map/ppermute | solution.py:17
  138.5 2.5 maximum_maximum_fusion.3
  141.0 2.3 copy.21
  143.3 2.4 copy.23
  145.7 3.8 %maximum_maximum_fusion = (f32[34,66,129]{2,1,0:T(8,128)S(1)}, f32[34,66,129]{2,1,0:T(8,128)S(1)}) fusion(f32[34,1,128]{2,1,0:T(1,128)} %copy-done.35, f32[1,64,128]{2,1,0:T(8,128)} %copy-done.30, f32[32,64,128]{2,1,0:T(8,128)S(1)} %get-tuple-element.32, f32[1,64,128]{2,1,0:T(8,128)} %copy-done.28, f32[34,1,128]{2,1,0:T(1,128)} %copy-done.33, ...), kind=kLoop, calls=%fused_computation.9 | loop fusion | flops 2894760 | bytes 3482688 | tf_op jit(solution)/shard_map/concatenate | solution.py:15
  149.8 9.8 %multiply_reduce_fusion.3 = (f32[]{:T(128)}, f32[]{:T(128)}, f32[32,64,128]{2,1,0:T(8,128)S(1)}) fusion(f32[32,64,128]{2,1,0:T(8,128)S(1)} %get-tuple-element.32, f32[32,64,128]{2,1,0:T(8,128)} %param.5, f32[34,66,129]{2,1,0:T(8,128)S(1)} %get-tuple-element.63, f32[34,66,130]{2,1,0:T(8,128)S(1)} %copy-done, f32[34,66,129]{2,1,0:T(8,128)S(1)} %get-tuple-element.62, ...), kind=kLoop, calls=%fused_computation.206 | loop fusion | flops 19136512 | bytes 43057160 | tf_op jit(solution)/shard_map/reduce_sum | solution.py:137
  159.9 2.8 collective-permute-start.12
  164.3 4.2 %collective-permute-done.13 = f32[1,64,128]{2,1,0:T(8,128)S(1)} collective-permute-done((f32[1,64,128]{2,1,0:T(8,128)S(1)}, f32[1,64,128]{2,1,0:T(8,128)S(1)}, u32[]{:S(2)}, u32[]{:S(2)}) %collective-permute-start.13) | collective-permute-done | bytes 32800 | tf_op jit(solution)/shard_map/ppermute | solution.py:19
  172.3 19.6 %all-reduce.2 = (f32[]{:T(128)}, f32[]{:T(128)}) all-reduce(f32[]{:T(128)} %get-tuple-element.8, f32[]{:T(128)} %get-tuple-element.7), channel_id=1, replica_groups=mesh['gx'=4,'gy'=2,'gz'=4] {'gy','gz'}, use_global_device_ids=true, to_apply=%region_1.0 | all-reduce | flops 2 | bytes 16 | tf_op jit(solution)/shard_map/psum | solution.py:135
  191.9 9.1 %all-reduce.5 = (f32[]{:T(128)}, f32[]{:T(128)}) all-reduce(f32[]{:T(128)} %get-tuple-element.21, f32[]{:T(128)} %get-tuple-element.22), channel_id=1, replica_groups=mesh['gx'=4,'gy'=2,'gz'=4] {'gx'}, use_global_device_ids=true, to_apply=%region_2.0 | all-reduce | flops 2 | bytes 16 | tf_op jit(solution)/shard_map/psum | solution.py:134
  205.5 2.4 copy.24
  207.9 2.4 copy.26
  211.5 5.1 %collective-permute-start.16 = (f32[34,66,1]{1,2,0:T(1,128)}, f32[34,66,1]{1,2,0:T(1,128)}, u32[]{:S(2)}, u32[]{:S(2)}) collective-permute-start(f32[34,66,1]{1,2,0:T(1,128)} %copy.24), channel_id=1, source_target_pairs={{0,1},{1,2},{2,3},{4,5},{5,6},{6,7},{8,9},{9,10},{10,11},{12,13},{... | collective-permute-start | bytes 26936 | tf_op jit(solution)/shard_map/ppermute | solution.py:17
  216.6 3.3 maximum_maximum_fusion.4
  222.2 2.4 copy.27
  224.6 4.2 %maximum_maximum_fusion.1 = (f32[34,66,129]{2,1,0:T(8,128)S(1)}, f32[34,66,129]{2,1,0:T(8,128)S(1)}) fusion(f32[34,1,128]{2,1,0:T(1,128)} %collective-permute-done.15, f32[1,64,128]{2,1,0:T(8,128)} %copy-done.26, f32[32,64,128]{2,1,0:T(8,128)} %copy-done.6, f32[1,64,128]{2,1,0:T(8,128)} %copy-done.24, f32[34,1,128]{2,1,0:T(1,128)} %collective-permute-done.14, ...), kind=kLoop, calls=%fused_computation.11 | loop fusion | flops 2894760 | bytes 3482688 | tf_op jit(solution)/shard_map/concatenate | solution.py:15
  229.4 9.6 %fusion.101 = (f32[32,64,128]{2,1,0:T(8,128)S(1)}, f32[32,64,128]{2,1,0:T(8,128)S(1)}) fusion(f32[32,64,128]{2,1,0:T(8,128)S(1)} %copy-done.18, f32[32,64,128]{2,1,0:T(8,128)S(1)} %copy-done.11, f32[]{:T(128)S(6)} %div.31, f32[34,66,129]{2,1,0:T(8,128)S(1)} %get-tuple-element.61, f32[34,66,130]{2,1,0:T(8,128)S(1)} %copy-done.1, ...), kind=kLoop, calls=%fused_computation.217 | loop fusion | flops 18874368 | bytes 45154308 | tf_op jit(solution)/shard_map/div | solution.py:139
  239.7 3.6 %collective-permute-start.18 = (f32[1,64,128]{2,1,0:T(8,128)}, f32[1,64,128]{2,1,0:T(8,128)}, u32[]{:S(2)}, u32[]{:S(2)}) collective-permute-start(f32[1,64,128]{2,1,0:T(8,128)} %get-tuple-element.76), channel_id=1, source_target_pairs={{0,8},{8,16},{16,24},{1,9},{9,17},{17,25},{2,10},{10,18},{18,26},{... | collective-permute-start | bytes 98312 | tf_op jit(solution)/shard_map/ppermute | solution.py:17
  245.8 14.7 %all-reduce.1 = (f32[]{:T(128)}, f32[]{:T(128)}) all-reduce(f32[]{:T(128)} %get-tuple-element.6, f32[]{:T(128)} %get-tuple-element.5), channel_id=1, replica_groups=mesh['gx'=4,'gy'=2,'gz'=4] {'gy','gz'}, use_global_device_ids=true, to_apply=%region_7.0 | all-reduce | flops 2 | bytes 16 | tf_op jit(solution)/shard_map/psum | solution.py:135
  260.5 10.8 %all-reduce.4 = (f32[]{:T(128)}, f32[]{:T(128)}) all-reduce(f32[]{:T(128)} %get-tuple-element.19, f32[]{:T(128)} %get-tuple-element.20), channel_id=1, replica_groups=mesh['gx'=4,'gy'=2,'gz'=4] {'gx'}, use_global_device_ids=true, to_apply=%region_8.0 | all-reduce | flops 2 | bytes 16 | tf_op jit(solution)/shard_map/psum | solution.py:134
  279.5 3.7 %multiply_reduce_fusion = f32[]{:T(128)} fusion(f32[32,64,128]{2,1,0:T(8,128)} %copy-done.10, f32[32,64,128]{2,1,0:T(8,128)} %param.5, f32[]{:T(128)S(6)} %div.33, f32[]{:T(128)S(6)} %div.35, f32[]{:T(128)S(6)} %div.31, f32[32,64,128]{2,1,0:T(8,128)} %copy-done.19, f32[32,64,128]{2,1,0:T(8,128)} %copy-done.6, f32[32,64,128]{2,1,0:T(8,128)} %get-tuple-element.33, ...), kind=kLoop, calls=%fused_computation.199 | loop fusion | flops 4456447 | bytes 6291472 | tf_op jit(solution)/shard_map/reduce_sum | solution.py:137
  286.0 2.4 copy.28
  288.3 2.4 copy.30
  292.0 5.1 %collective-permute-start.22 = (f32[34,66,1]{1,2,0:T(1,128)}, f32[34,66,1]{1,2,0:T(1,128)}, u32[]{:S(2)}, u32[]{:S(2)}) collective-permute-start(f32[34,66,1]{1,2,0:T(1,128)} %copy.28), channel_id=1, source_target_pairs={{0,1},{1,2},{2,3},{4,5},{5,6},{6,7},{8,9},{9,10},{10,11},{12,13},{... | collective-permute-start | bytes 26936 | tf_op jit(solution)/shard_map/ppermute | solution.py:17
  297.1 3.2 maximum_maximum_fusion.5
  302.6 2.4 copy.31
  305.0 4.1 %maximum_maximum_fusion.2 = (f32[34,66,129]{2,1,0:T(8,128)S(1)}, f32[34,66,129]{2,1,0:T(8,128)S(1)}) fusion(f32[34,1,128]{2,1,0:T(1,128)} %copy-done.34, f32[1,64,128]{2,1,0:T(8,128)} %collective-permute-done.19, f32[32,64,128]{2,1,0:T(8,128)} %copy-done.14, f32[1,64,128]{2,1,0:T(8,128)} %collective-permute-done.18, f32[34,1,128]{2,1,0:T(1,128)} %copy-done.32, ...), kind=kLoop, calls=%fused_computation.13 | loop fusion | flops 2894760 | bytes 3482688 | tf_op jit(solution)/shard_map/concatenate | solution.py:15
  309.8 10.8 %fusion.5 = f32[]{:T(128)} fusion(f32[34,66,129]{2,1,0:T(8,128)S(1)} %get-tuple-element.59, f32[34,66,129]{2,1,0:T(8,128)S(1)} %get-tuple-element.58, f32[34,65,128]{2,1,0:T(8,128)} %get-tuple-element.65, f32[34,65,128]{2,1,0:T(8,128)} %get-tuple-element.64, f32[32,64,128]{2,1,0:T(8,128)} %get-tuple-element.39, f32[32,64,128]{2,1,0:T(8,128)S(1)} %copy-done.16, ...), kind=kLoop, calls=%fused_computation.30 | loop fusion | flops 22020096 | bytes 46202896 | tf_op jit(solution)/shard_map/reduce_sum | solution.py:137
  320.6 15.9 %all-reduce = (f32[]{:T(128)}, f32[]{:T(128)}) all-reduce(f32[]{:T(128)} %multiply_reduce_fusion, f32[]{:T(128)} %fusion.5), channel_id=1, replica_groups=mesh['gx'=4,'gy'=2,'gz'=4] {'gy','gz'}, use_global_device_ids=true, to_apply=%region_13.0 | all-reduce | flops 2 | bytes 16 | tf_op jit(solution)/shard_map/psum | solution.py:135
  336.5 10.2 %all-reduce.3 = (f32[]{:T(128)}, f32[]{:T(128)}) all-reduce(f32[]{:T(128)} %get-tuple-element.17, f32[]{:T(128)} %get-tuple-element.18), channel_id=1, replica_groups=mesh['gx'=4,'gy'=2,'gz'=4] {'gx'}, use_global_device_ids=true, to_apply=%region_14.0 | all-reduce | flops 2 | bytes 16 | tf_op jit(solution)/shard_map/psum | solution.py:134
  350.3 3.8 %multiply_add_fusion.1 = f32[32,64,128]{2,1,0:T(8,128)} fusion(f32[32,64,128]{2,1,0:T(8,128)S(1)} %get-tuple-element.32, f32[]{:T(128)S(6)} %div.37, f32[]{:T(128)S(6)} %div.39, f32[]{:T(128)S(6)} %div.33, f32[]{:T(128)S(6)} %div.35, f32[]{:T(128)S(6)} %div.31, f32[32,64,128]{2,1,0:T(8,128)} %copy-done.6, f32[32,64,128]{2,1,0:T(8,128)} %get-tuple-element.33, ...), kind=kLoop, calls=%fused_computation.198 | loop fusion | flops 4718592 | bytes 6291476 | tf_op jit(solution)/shard_map/add | solution.py:155
  (130 shorter events, 50.9 us)
Async XLA Ops:
  7.4 7.4 %copy-start.13 = (f32[7,32,64,128]{3,2,1,0:T(8,128)}, f32[7,32,64,128]{3,2,1,0:T(8,128)S(1)}, u32[]{:S(2)}) copy-start(f32[7,32,64,128]{3,2,1,0:T(8,128)S(1)} %multiply_add_fusion) | copy-start | bytes 22020100
  7.5 9.0 %collective-permute-start = (f32[6,1,64,128]{3,2,1,0:T(8,128)S(1)}, f32[6,1,64,128]{3,2,1,0:T(8,128)S(1)}, u32[]{:S(2)}, u32[]{:S(2)}) collective-permute-start(f32[6,1,64,128]{3,2,1,0:T(8,128)S(1)} %get-tuple-element.48), channel_id=1, source_target_pairs={{0,8},{8,16},{16,24},{1,9},{9,17},{17,25},{2,10},{10,18},{18,26},{... | collective-permute-start | bytes 589832 | tf_op jit(solution)/shard_map/ppermute | solution.py:17
  12.4 10.3 %collective-permute-start.1 = (f32[6,1,64,128]{3,2,1,0:T(8,128)S(1)}, f32[6,1,64,128]{3,2,1,0:T(8,128)S(1)}, u32[]{:S(2)}, u32[]{:S(2)}) collective-permute-start(f32[6,1,64,128]{3,2,1,0:T(8,128)S(1)} %get-tuple-element.49), channel_id=1, source_target_pairs={{8,0},{16,8},{24,16},{9,1},{17,9},{25,17},{10,2},{18,10},{26,18},{... | collective-permute-start | bytes 589832 | tf_op jit(solution)/shard_map/ppermute | solution.py:19
  14.8 12.5 %copy-start.9 = (f32[6,32,64,128]{3,2,1,0:T(8,128)}, f32[6,32,64,128]{3,2,1,0:T(8,128)S(1)}, u32[]{:S(2)}) copy-start(f32[6,32,64,128]{3,2,1,0:T(8,128)S(1)} %slice.740) | copy-start | bytes 18874372
  22.8 2.6 collective-permute-start.2
  24.1 3.2 collective-permute-start.3
  48.6 10.1 %collective-permute-start.4 = (f32[6,34,66,1]{2,3,1,0:T(1,128)S(1)}, f32[6,34,66,1]{2,3,1,0:T(1,128)S(1)}, u32[]{:S(2)}, u32[]{:S(2)}) collective-permute-start(f32[6,34,66,1]{2,3,1,0:T(1,128)S(1)} %copy.16), channel_id=1, source_target_pairs={{0,1},{1,2},{2,3},{4,5},{5,6},{6,7},{8,9},{9,10},{10,11},{12,13},{... | collective-permute-start | bytes 161576 | tf_op jit(solution)/shard_map/ppermute | solution.py:17
  57.2 6.6 %collective-permute-start.5 = (f32[6,34,66,1]{2,3,1,0:T(1,128)S(1)}, f32[6,34,66,1]{2,3,1,0:T(1,128)S(1)}, u32[]{:S(2)}, u32[]{:S(2)}) collective-permute-start(f32[6,34,66,1]{2,3,1,0:T(1,128)S(1)} %copy.17), channel_id=1, source_target_pairs={{1,0},{2,1},{3,2},{5,4},{6,5},{7,6},{9,8},{10,9},{11,10},{13,12},{... | collective-permute-start | bytes 161576 | tf_op jit(solution)/shard_map/ppermute | solution.py:19
  110.7 5.0 %collective-permute-start.6 = (f32[1,64,128]{2,1,0:T(8,128)S(1)}, f32[1,64,128]{2,1,0:T(8,128)S(1)}, u32[]{:S(2)}, u32[]{:S(2)}) collective-permute-start(f32[1,64,128]{2,1,0:T(8,128)S(1)} %get-tuple-element.80), channel_id=1, source_target_pairs={{0,8},{8,16},{16,24},{1,9},{9,17},{17,25},{2,10},{10,18},{18,26},{... | collective-permute-start | bytes 98312 | tf_op jit(solution)/shard_map/ppermute | solution.py:17
  114.1 5.8 %collective-permute-start.7 = (f32[1,64,128]{2,1,0:T(8,128)S(1)}, f32[1,64,128]{2,1,0:T(8,128)S(1)}, u32[]{:S(2)}, u32[]{:S(2)}) collective-permute-start(f32[1,64,128]{2,1,0:T(8,128)S(1)} %get-tuple-element.81), channel_id=1, source_target_pairs={{8,0},{16,8},{24,16},{9,1},{17,9},{25,17},{10,2},{18,10},{26,18},{... | collective-permute-start | bytes 98312 | tf_op jit(solution)/shard_map/ppermute | solution.py:19
  115.7 8.6 %copy-start.28 = (f32[1,64,128]{2,1,0:T(8,128)}, f32[1,64,128]{2,1,0:T(8,128)S(1)}, u32[]{:S(2)}) copy-start(f32[1,64,128]{2,1,0:T(8,128)S(1)} %collective-permute-done.6) | copy-start | bytes 98308
  119.9 4.4 %copy-start.30 = (f32[1,64,128]{2,1,0:T(8,128)}, f32[1,64,128]{2,1,0:T(8,128)S(1)}, u32[]{:S(2)}) copy-start(f32[1,64,128]{2,1,0:T(8,128)S(1)} %collective-permute-done.7) | copy-start | bytes 98308
  119.9 2.6 collective-permute-start.8
  121.2 3.1 collective-permute-start.9
  131.6 11.6 %collective-permute-start.11 = (f32[34,66,1]{1,2,0:T(1,128)}, f32[34,66,1]{1,2,0:T(1,128)}, u32[]{:S(2)}, u32[]{:S(2)}) collective-permute-start(f32[34,66,1]{1,2,0:T(1,128)} %copy.22), channel_id=1, source_target_pairs={{1,0},{2,1},{3,2},{5,4},{6,5},{7,6},{9,8},{10,9},{11,10},{13,12},{... | collective-permute-start | bytes 26936 | tf_op jit(solution)/shard_map/ppermute | solution.py:19
  132.9 8.1 %collective-permute-start.10 = (f32[34,66,1]{1,2,0:T(1,128)}, f32[34,66,1]{1,2,0:T(1,128)}, u32[]{:S(2)}, u32[]{:S(2)}) collective-permute-start(f32[34,66,1]{1,2,0:T(1,128)} %copy.20), channel_id=1, source_target_pairs={{0,1},{1,2},{2,3},{4,5},{5,6},{6,7},{8,9},{9,10},{10,11},{12,13},{... | collective-permute-start | bytes 26936 | tf_op jit(solution)/shard_map/ppermute | solution.py:17
  145.6 4.2 %copy-start.22 = (f32[32,64,128]{2,1,0:T(8,128)S(1)}, f32[32,64,128]{2,1,0:T(8,128)}, u32[]{:S(2)}) copy-start(f32[32,64,128]{2,1,0:T(8,128)} %get-tuple-element.36) | copy-start | bytes 3145732
  145.7 4.2 %copy-start.29 = (f32[1,64,128]{2,1,0:T(8,128)S(1)}, f32[1,64,128]{2,1,0:T(8,128)}, u32[]{:S(2)}) copy-start(f32[1,64,128]{2,1,0:T(8,128)} %copy-done.28) | copy-start | bytes 98308
  149.8 9.8 %copy-start.17 = (f32[32,64,128]{2,1,0:T(8,128)S(1)}, f32[32,64,128]{2,1,0:T(8,128)}, u32[]{:S(2)}) copy-start(f32[32,64,128]{2,1,0:T(8,128)} %get-tuple-element.33) | copy-start | bytes 3145732
  159.7 9.5 %copy-start.10 = (f32[32,64,128]{2,1,0:T(8,128)}, f32[32,64,128]{2,1,0:T(8,128)S(1)}, u32[]{:S(2)}) copy-start(f32[32,64,128]{2,1,0:T(8,128)S(1)} %get-tuple-element.31) | copy-start | bytes 3145732
  159.8 8.7 %copy-start.6 = (f32[32,64,128]{2,1,0:T(8,128)}, f32[32,64,128]{2,1,0:T(8,128)S(1)}, u32[]{:S(2)}) copy-start(f32[32,64,128]{2,1,0:T(8,128)S(1)} %div.32) | copy-start | bytes 3145732
  159.9 4.4 %collective-permute-start.12 = (f32[1,64,128]{2,1,0:T(8,128)S(1)}, f32[1,64,128]{2,1,0:T(8,128)S(1)}, u32[]{:S(2)}, u32[]{:S(2)}) collective-permute-start(f32[1,64,128]{2,1,0:T(8,128)S(1)} %get-tuple-element.78), channel_id=1, source_target_pairs={{0,8},{8,16},{16,24},{1,9},{9,17},{17,25},{2,10},{10,18},{18,26},{... | collective-permute-start | bytes 98312 | tf_op jit(solution)/shard_map/ppermute | solution.py:17
  162.7 5.8 %collective-permute-start.13 = (f32[1,64,128]{2,1,0:T(8,128)S(1)}, f32[1,64,128]{2,1,0:T(8,128)S(1)}, u32[]{:S(2)}, u32[]{:S(2)}) collective-permute-start(f32[1,64,128]{2,1,0:T(8,128)S(1)} %get-tuple-element.79), channel_id=1, source_target_pairs={{8,0},{16,8},{24,16},{9,1},{17,9},{25,17},{10,2},{18,10},{26,18},{... | collective-permute-start | bytes 98312 | tf_op jit(solution)/shard_map/ppermute | solution.py:19
  164.3 4.9 %copy-start.24 = (f32[1,64,128]{2,1,0:T(8,128)}, f32[1,64,128]{2,1,0:T(8,128)S(1)}, u32[]{:S(2)}) copy-start(f32[1,64,128]{2,1,0:T(8,128)S(1)} %collective-permute-done.12) | copy-start | bytes 98308
  169.1 33.1 %collective-permute-start.14 = (f32[34,1,128]{2,1,0:T(1,128)}, f32[34,1,128]{2,1,0:T(1,128)}, u32[]{:S(2)}, u32[]{:S(2)}) collective-permute-start(f32[34,1,128]{2,1,0:T(1,128)} %get-tuple-element.70), channel_id=1, source_target_pairs={{0,4},{1,5},{2,6},{3,7},{8,12},{9,13},{10,14},{11,15},{16,20},{17,... | collective-permute-start | bytes 52232 | tf_op jit(solution)/shard_map/ppermute | solution.py:17
  171.0 31.2 %collective-permute-start.15 = (f32[34,1,128]{2,1,0:T(1,128)}, f32[34,1,128]{2,1,0:T(1,128)}, u32[]{:S(2)}, u32[]{:S(2)}) collective-permute-start(f32[34,1,128]{2,1,0:T(1,128)} %get-tuple-element.71), channel_id=1, source_target_pairs={{4,0},{5,1},{6,2},{7,3},{12,8},{13,9},{14,10},{15,11},{20,16},{21,... | collective-permute-start | bytes 52232 | tf_op jit(solution)/shard_map/ppermute | solution.py:19
  210.2 12.0 %collective-permute-start.17 = (f32[34,66,1]{1,2,0:T(1,128)}, f32[34,66,1]{1,2,0:T(1,128)}, u32[]{:S(2)}, u32[]{:S(2)}) collective-permute-start(f32[34,66,1]{1,2,0:T(1,128)} %copy.26), channel_id=1, source_target_pairs={{1,0},{2,1},{3,2},{5,4},{6,5},{7,6},{9,8},{10,9},{11,10},{13,12},{... | collective-permute-start | bytes 26936 | tf_op jit(solution)/shard_map/ppermute | solution.py:19
  211.5 8.4 %collective-permute-start.16 = (f32[34,66,1]{1,2,0:T(1,128)}, f32[34,66,1]{1,2,0:T(1,128)}, u32[]{:S(2)}, u32[]{:S(2)}) collective-permute-start(f32[34,66,1]{1,2,0:T(1,128)} %copy.24), channel_id=1, source_target_pairs={{0,1},{1,2},{2,3},{4,5},{5,6},{6,7},{8,9},{9,10},{10,11},{12,13},{... | collective-permute-start | bytes 26936 | tf_op jit(solution)/shard_map/ppermute | solution.py:17
  224.6 4.2 %copy-start.1 = (f32[34,66,130]{2,1,0:T(8,128)S(1)}, f32[34,66,130]{2,1,0:T(8,128)}, u32[]{:S(2)}) copy-start(f32[34,66,130]{2,1,0:T(8,128)} %get-tuple-element.41) | copy-start | bytes 3500644
  224.6 4.2 %copy-start.4 = (f32[34,66,130]{2,1,0:T(8,128)S(1)}, f32[34,66,130]{2,1,0:T(8,128)}, u32[]{:S(2)}) copy-start(f32[34,66,130]{2,1,0:T(8,128)} %get-tuple-element.42) | copy-start | bytes 3500644
  224.6 4.2 %copy-start.7 = (f32[32,64,128]{2,1,0:T(8,128)S(1)}, f32[32,64,128]{2,1,0:T(8,128)}, u32[]{:S(2)}) copy-start(f32[32,64,128]{2,1,0:T(8,128)} %copy-done.6) | copy-start | bytes 3145732
  224.6 4.5 %copy-start.11 = (f32[32,64,128]{2,1,0:T(8,128)S(1)}, f32[32,64,128]{2,1,0:T(8,128)}, u32[]{:S(2)}) copy-start(f32[32,64,128]{2,1,0:T(8,128)} %copy-done.10) | copy-start | bytes 3145732
  224.6 4.8 %copy-start.18 = (f32[32,64,128]{2,1,0:T(8,128)S(1)}, f32[32,64,128]{2,1,0:T(8,128)}, u32[]{:S(2)}) copy-start(f32[32,64,128]{2,1,0:T(8,128)} %get-tuple-element.33) | copy-start | bytes 3145732
  224.6 4.8 %copy-start.25 = (f32[1,64,128]{2,1,0:T(8,128)S(1)}, f32[1,64,128]{2,1,0:T(8,128)}, u32[]{:S(2)}) copy-start(f32[1,64,128]{2,1,0:T(8,128)} %copy-done.24) | copy-start | bytes 98308
  224.6 4.8 %copy-start.27 = (f32[1,64,128]{2,1,0:T(8,128)S(1)}, f32[1,64,128]{2,1,0:T(8,128)}, u32[]{:S(2)}) copy-start(f32[1,64,128]{2,1,0:T(8,128)} %copy-done.26) | copy-start | bytes 98308
  229.4 15.1 %copy-start.23 = (f32[32,64,128]{2,1,0:T(8,128)S(1)}, f32[32,64,128]{2,1,0:T(8,128)}, u32[]{:S(2)}) copy-start(f32[32,64,128]{2,1,0:T(8,128)} %param.5) | copy-start | bytes 3145732
  239.0 6.8 %copy-start.14 = (f32[32,64,128]{2,1,0:T(8,128)}, f32[32,64,128]{2,1,0:T(8,128)S(1)}, u32[]{:S(2)}) copy-start(f32[32,64,128]{2,1,0:T(8,128)S(1)} %get-tuple-element.29) | copy-start | bytes 3145732
  239.0 6.8 %copy-start.19 = (f32[32,64,128]{2,1,0:T(8,128)}, f32[32,64,128]{2,1,0:T(8,128)S(1)}, u32[]{:S(2)}) copy-start(f32[32,64,128]{2,1,0:T(8,128)S(1)} %get-tuple-element.30) | copy-start | bytes 3145732
  239.7 36.0 %collective-permute-start.18 = (f32[1,64,128]{2,1,0:T(8,128)}, f32[1,64,128]{2,1,0:T(8,128)}, u32[]{:S(2)}, u32[]{:S(2)}) collective-permute-start(f32[1,64,128]{2,1,0:T(8,128)} %get-tuple-element.76), channel_id=1, source_target_pairs={{0,8},{8,16},{16,24},{1,9},{9,17},{17,25},{2,10},{10,18},{18,26},{... | collective-permute-start | bytes 98312 | tf_op jit(solution)/shard_map/ppermute | solution.py:17
  243.2 32.5 %collective-permute-start.19 = (f32[1,64,128]{2,1,0:T(8,128)}, f32[1,64,128]{2,1,0:T(8,128)}, u32[]{:S(2)}, u32[]{:S(2)}) collective-permute-start(f32[1,64,128]{2,1,0:T(8,128)} %get-tuple-element.77), channel_id=1, source_target_pairs={{8,0},{16,8},{24,16},{9,1},{17,9},{25,17},{10,2},{18,10},{26,18},{... | collective-permute-start | bytes 98312 | tf_op jit(solution)/shard_map/ppermute | solution.py:19
  276.7 6.5 %collective-permute-start.20 = (f32[34,1,128]{2,1,0:T(1,128)S(1)}, f32[34,1,128]{2,1,0:T(1,128)S(1)}, u32[]{:S(2)}, u32[]{:S(2)}) collective-permute-start(f32[34,1,128]{2,1,0:T(1,128)S(1)} %get-tuple-element.66), channel_id=1, source_target_pairs={{0,4},{1,5},{2,6},{3,7},{8,12},{9,13},{10,14},{11,15},{16,20},{17,... | collective-permute-start | bytes 52232 | tf_op jit(solution)/shard_map/ppermute | solution.py:17
  278.0 5.2 %copy-start.15 = (f32[32,64,128]{2,1,0:T(8,128)S(1)}, f32[32,64,128]{2,1,0:T(8,128)}, u32[]{:S(2)}) copy-start(f32[32,64,128]{2,1,0:T(8,128)} %copy-done.14) | copy-start | bytes 3145732
  278.1 5.2 %collective-permute-start.21 = (f32[34,1,128]{2,1,0:T(1,128)S(1)}, f32[34,1,128]{2,1,0:T(1,128)S(1)}, u32[]{:S(2)}, u32[]{:S(2)}) collective-permute-start(f32[34,1,128]{2,1,0:T(1,128)S(1)} %get-tuple-element.67), channel_id=1, source_target_pairs={{4,0},{5,1},{6,2},{7,3},{12,8},{13,9},{14,10},{15,11},{20,16},{21,... | collective-permute-start | bytes 52232 | tf_op jit(solution)/shard_map/ppermute | solution.py:19
  290.7 11.9 %collective-permute-start.23 = (f32[34,66,1]{1,2,0:T(1,128)}, f32[34,66,1]{1,2,0:T(1,128)}, u32[]{:S(2)}, u32[]{:S(2)}) collective-permute-start(f32[34,66,1]{1,2,0:T(1,128)} %copy.30), channel_id=1, source_target_pairs={{1,0},{2,1},{3,2},{5,4},{6,5},{7,6},{9,8},{10,9},{11,10},{13,12},{... | collective-permute-start | bytes 26936 | tf_op jit(solution)/shard_map/ppermute | solution.py:19
  292.0 8.4 %collective-permute-start.22 = (f32[34,66,1]{1,2,0:T(1,128)}, f32[34,66,1]{1,2,0:T(1,128)}, u32[]{:S(2)}, u32[]{:S(2)}) collective-permute-start(f32[34,66,1]{1,2,0:T(1,128)} %copy.28), channel_id=1, source_target_pairs={{0,1},{1,2},{2,3},{4,5},{5,6},{6,7},{8,9},{9,10},{10,11},{12,13},{... | collective-permute-start | bytes 26936 | tf_op jit(solution)/shard_map/ppermute | solution.py:17
  305.0 4.2 %copy-start.8 = (f32[32,64,128]{2,1,0:T(8,128)S(1)}, f32[32,64,128]{2,1,0:T(8,128)}, u32[]{:S(2)}) copy-start(f32[32,64,128]{2,1,0:T(8,128)} %copy-done.6) | copy-start | bytes 3145732
  305.0 4.5 %copy-start.12 = (f32[32,64,128]{2,1,0:T(8,128)S(1)}, f32[32,64,128]{2,1,0:T(8,128)}, u32[]{:S(2)}) copy-start(f32[32,64,128]{2,1,0:T(8,128)} %copy-done.10) | copy-start | bytes 3145732
  305.0 4.8 %copy-start.16 = (f32[32,64,128]{2,1,0:T(8,128)S(1)}, f32[32,64,128]{2,1,0:T(8,128)}, u32[]{:S(2)}) copy-start(f32[32,64,128]{2,1,0:T(8,128)} %copy-done.14) | copy-start | bytes 3145732
  (12 other events, 38.2 us)
